TPU v7x, 32 devices: a whole 2x2x4 slice. The times are simulated.
32 devices in a mesh: row: 8 (over z, y), col: 4 (over x, core).
Axes of the slice: x: 2, y: 2, z: 4, core: 2. Of those that a mesh axis runs over, the one named last changes fastest.
Arguments:
- matrix: float32 [4, 8, 512, 8, 4, 512], P(None, 'row', None, None, 'col'), may hold values from -30 to 30, as said below
Outputs:
- factored: float32 [4, 8, 512, 8, 4, 512], P(None, 'row', None, None, 'col')
Inputs may be any that keep to these rules, and one draw needn't show every extreme that they name: matrix is symmetric, positive definite and well conditioned.
All inputs are finite; a program needn't handle non-finite values.
Results may differ from a plain program's by a relative error of at most 0.00013.
Values sent between devices are 32-bit elements; how exact they have to be, the bound alone decides.
A program may use at most 192 MiB of HBM per device.

v0:
```python
import jax
import jax.numpy as jnp
from jax import lax
from jax.sharding import PartitionSpec as P

NB = 512
STEPS = 2


def spread(value, axis, source):
    kept = jnp.where(lax.axis_index(axis) == source, value, 0).astype(value.dtype)
    return lax.psum(kept, axis)


def trailing_product(column_panel, transposed):
    return jnp.einsum(
        "tan,sbn->tasb",
        column_panel,
        transposed,
        precision=lax.Precision.HIGHEST,
        preferred_element_type=jnp.float32,
    )


def shards(matrix):
    local_rows = matrix.shape[0]
    local_cols = matrix.shape[3]
    blocks = matrix.reshape(local_rows, NB, local_cols, NB)
    row_count = lax.axis_size("row")
    column_count = lax.axis_size("col")
    group_size = row_count // column_count
    row_place = lax.axis_index("row")
    column_place = lax.axis_index("col")
    tile_rows = jnp.arange(local_rows, dtype=jnp.int32) * row_count + row_place
    tile_columns = jnp.arange(local_cols, dtype=jnp.int32) * column_count + column_place
    anchor = jnp.int32(0)
    for step in range(STEPS):
        root_row = step % row_count
        factor_local_row = step // row_count
        root_col = step % column_count
        factor_local_col = step // column_count
        corner = blocks[factor_local_row, :, factor_local_col, :]
        owner = (row_place == root_row) & (column_place == root_col)
        identity = jnp.eye(NB, dtype=jnp.float32)
        chosen = jnp.where(owner, corner, identity)
        factor_local = jnp.linalg.cholesky(chosen)
        factor_diag_block = spread(factor_local, "row", root_row)
        source = blocks[:, :, factor_local_col, :]
        solved = jax.scipy.linalg.solve_triangular(
            factor_diag_block, source.reshape(local_rows * NB, NB).T, lower=True
        ).T
        solved = solved.reshape(local_rows, NB, NB)
        panel_local = jnp.where((tile_rows > step)[:, None, None], solved, 0.0)
        factor_column_panel = spread(panel_local, "col", root_col)
        empty = jnp.zeros((local_rows, group_size, NB, NB), jnp.float32)
        slot_index = row_place // column_count
        holder = row_place % column_count == column_place
        contribution = jnp.where(holder, factor_column_panel, 0.0)
        filled = lax.dynamic_update_slice(
            empty, contribution[:, None], (anchor, slot_index, anchor, anchor)
        )
        gathered = lax.psum(filled, "row")
        transposed = gathered.reshape(local_cols, NB, NB)
        diag_block, column_panel, transposed = (factor_diag_block, factor_column_panel, transposed)
        write_blocks = blocks
        local_row = step // row_count
        local_col = step // column_count
        column_now = write_blocks[:, :, local_col, :]
        owns_col = column_place == step % column_count
        row_after = (tile_rows > step)[:, None, None]
        row_hit = (tile_rows == step)[:, None, None]
        new_column = jnp.where(
            row_after, column_panel, jnp.where(row_hit, diag_block[None], column_now)
        )
        new_column = jnp.where(owns_col, new_column, column_now)
        write_blocks = write_blocks.at[:, :, local_col, :].set(new_column)
        row_now = write_blocks[local_row]
        owns_row = row_place == step % row_count
        zero_cols = (tile_columns > step)[None, :, None]
        new_row = jnp.where(owns_row & zero_cols, 0.0, row_now)
        blocks = write_blocks.at[local_row].set(new_row)
        blocks = blocks - trailing_product(column_panel, transposed)
    return blocks.reshape(matrix.shape)


def solution(mesh):
    in_specs = (P(None, "row", None, None, "col", None),)
    out_specs = P(None, "row", None, None, "col", None)
    return jax.shard_map(shards, mesh=mesh, in_specs=in_specs, out_specs=out_specs, check_vma=False)
```

profile of v0, /device:TPU:0, one launch (start us, length us, event | category | flops | bytes accessed | tf_op | source)
XLA Modules:
  0.0 1563.9 jit_solution(13661579687502120736)
XLA Ops:
  6.5 78.2 %copy.17 = f32[4,1,512,8,1,512]{2,5,3,0,4,1:T(8,128)} copy(f32[4,1,512,8,1,512]{5,4,3,2,1,0:T(1,128)} %param.12) | data formatting | bytes 67108864 | tf_op args[0]
  87.9 11.7 cholesky.286
  99.7 9.8 custom-call.27
  110.3 11.7 cholesky.305
  122.0 10.0 custom-call.28
  132.7 11.7 cholesky.326
  155.6 11.7 cholesky.343
  182.8 78.7 %copy.42 = f32[4,1,512,8,1,512]{2,5,0,3,1,4:T(8,128)} copy(f32[4,1,512,8,1,512]{5,4,3,2,1,0:T(1,128)} %param.12) | data formatting | bytes 67108864 | tf_op jit(solution)/shard_map/reshape | solution.py:28
  280.5 39.3 %custom-call.30 = f32[4,128,128]{1,2,0:T(8,128)S(1)} custom-call(f32[4,128,128]{2,1,0:T(8,128)S(1)} %get-tuple-element.69), custom_call_target="InvertDiagBlocksLowerTriangular" | custom-call | tf_op jit(solution)/shard_map/jit(_solve_triangular)/triangular_solve | solution.py:49
  355.9 88.4 %all-reduce.10.cloned.1.call-done = f32[4,512,512]{1,2,0:T(8,128)} async-done(((f32[4,512,512]{1,2,0:T(8,128)}), f32[4,512,512]{1,2,0:T(8,128)}) %all-reduce.10.cloned.1.call-update) | async-done | bytes 4194320 | tf_op jit(solution)/shard_map/psum | solution.py:12
  477.5 253.1 %all-reduce.12.cloned.1.call-done = f32[8,512,512]{2,1,0:T(8,128)} async-done(((f32[8,512,512]{2,1,0:T(8,128)}), f32[8,512,512]{2,1,0:T(8,128)}) %all-reduce.12.cloned.1.call-update) | async-done | bytes 8388624 | tf_op jit(solution)/shard_map/psum | solution.py:62
  730.6 63.0 %convolution_subtract_fusion = f32[4,512,8,512]{1,3,2,0:T(8,128)} fusion(f32[4,512,8,512]{1,3,2,0:T(8,128)} %fusion.1, f32[8,512,512]{2,1,0:T(8,128)} %all-reduce.12.cloned.1.call-done, f32[4,512,512]{1,2,0:T(8,128)} %all-reduce.10.cloned.1.call-done), kind=kOutput, calls=%fused_computation.5 | convolution fusion | flops 51547996160 | bytes 79691776 | tf_op jit(solution)/shard_map/tan,sbn->tasb/dot_general | solution.py:16
  796.7 11.7 cholesky.358
  808.6 9.8 custom-call.31
  819.1 11.7 cholesky.377
  832.2 10.2 custom-call.32
  843.0 11.7 cholesky.398
  865.9 11.7 cholesky.415
  894.3 65.6 %all-reduce.14.cloned.1.call-done = f32[512,512]{1,0:T(8,128)} async-done(((f32[512,512]{1,0:T(8,128)}), f32[512,512]{1,0:T(8,128)}) %all-reduce.14.cloned.1.call-update) | async-done | bytes 1048592 | tf_op jit(solution)/shard_map/psum | solution.py:12
  969.0 39.3 %custom-call.34 = f32[4,128,128]{1,2,0:T(8,128)S(1)} custom-call(f32[4,128,128]{2,1,0:T(8,128)S(1)} %get-tuple-element.70), custom_call_target="InvertDiagBlocksLowerTriangular" | custom-call | tf_op jit(solution)/shard_map/jit(_solve_triangular)/triangular_solve | solution.py:49
  1044.2 85.2 %all-reduce.16.cloned.1.call-done = f32[4,512,512]{1,2,0:T(8,128)} async-done(((f32[4,512,512]{1,2,0:T(8,128)}), f32[4,512,512]{1,2,0:T(8,128)}) %all-reduce.16.cloned.1.call-update) | async-done | bytes 4194320 | tf_op jit(solution)/shard_map/psum | solution.py:12
  1162.7 253.0 %all-reduce.18.cloned.1.call-done = f32[8,512,512]{2,1,0:T(8,128)} async-done(((f32[8,512,512]{2,1,0:T(8,128)}), f32[8,512,512]{2,1,0:T(8,128)}) %all-reduce.18.cloned.1.call-update) | async-done | bytes 8388624 | tf_op jit(solution)/shard_map/psum | solution.py:62
  1415.8 62.8 %subtract_bitcast_fusion = f32[4,1,512,8,1,512]{2,5,3,0,4,1:T(8,128)} fusion(f32[4,512,8,512]{1,3,2,0:T(8,128)} %fusion, f32[8,512,512]{2,1,0:T(8,128)} %all-reduce.18.cloned.1.call-done, f32[4,512,512]{1,2,0:T(8,128)} %all-reduce.16.cloned.1.call-done), kind=kOutput, calls=%fused_computation.4 | convolution fusion | flops 51547996160 | bytes 79691776 | tf_op jit(solution)/shard_map/tan,sbn->tasb/dot_general | solution.py:16
  1478.5 78.2 %copy.37 = f32[4,1,512,8,1,512]{5,4,3,2,1,0:T(1,128)} copy(f32[4,1,512,8,1,512]{2,5,3,0,4,1:T(8,128)} %subtract_bitcast_fusion) | data formatting | bytes 67108864 | tf_op jit(solution)/shard_map/reshape | solution.py:83
  (148 shorter events, 230.9 us)
Async XLA Ops:
  6.5 264.9 %all-reduce.8.cloned.1.call-start = ((), (), s32[]{:S(2)}) async-start(), calls=%async_computation | async-start | bytes 2097152 | tf_op jit(solution)/shard_map/psum | solution.py:12
  182.8 261.4 %all-reduce.10.cloned.1.call-start = ((), (), s32[]{:S(2)}) async-start(), calls=%async_computation.1 | async-start | bytes 8388608 | tf_op jit(solution)/shard_map/psum | solution.py:12
  319.8 6.6 copy-start.2
  355.8 374.8 %all-reduce.12.cloned.1.call-start = ((), (), s32[]{:S(2)}) async-start(), calls=%async_computation.2 | async-start | bytes 16777216 | tf_op jit(solution)/shard_map/psum | solution.py:62
  454.1 4.3 copy-start.1
  460.8 1.2 copy-start.4
  460.8 499.0 %all-reduce.14.cloned.1.call-start = ((), (), s32[]{:S(2)}) async-start(), calls=%async_computation.3 | async-start | bytes 2097152 | tf_op jit(solution)/shard_map/psum | solution.py:12
  882.2 247.2 %all-reduce.16.cloned.1.call-start = ((), (), s32[]{:S(2)}) async-start(), calls=%async_computation.4 | async-start | bytes 8388608 | tf_op jit(solution)/shard_map/psum | solution.py:12
  1008.4 6.6 copy-start.3
  1044.2 371.6 %all-reduce.18.cloned.1.call-start = ((), (), s32[]{:S(2)}) async-start(), calls=%async_computation.5 | async-start | bytes 16777216 | tf_op jit(solution)/shard_map/psum | solution.py:62
  1139.3 4.3 copy-start
  1146.0 1.2 copy-start.5
Sparse Core Ops, SparseCore 0:
  182.9 81.0 all-reduce.7
  355.9 88.2 all-reduce.9
  460.9 269.6 all-reduce.11
  882.3 77.4 all-reduce.13
  1044.3 85.0 all-reduce.15
  1146.1 269.5 all-reduce.17
where the time goes:
time: 1580 us; the launch traced here: 1560 us
  waiting for transfers between devices  745 us (47%)
  local copies, waits for them, and re-layouts  321 us (20%)
  other arithmetic  302 us (19%)
  matrix products  165 us (10%)
  between operations  30 us (2%)
    psum x2, waiting for transfers between devices, shards(): gathered = lax.psum(filled, 'row')  506 us
    psum x4, waiting for transfers between devices, spread(): return lax.psum(kept, axis)  239 us
    another operation x29, other arithmetic, shards(): factor_local = jnp.linalg.cholesky(chosen)  158 us
    dot_general x2, matrix products, trailing_product(): jnp.einsum('tan,sbn->tasb', column_panel, transposed, precision=lax.Preci...  126 us
    another operation x5, other arithmetic, shards(): jax.scipy.linalg.solve_triangular(factor_diag_block, source.reshape(local...  81.3 us
    unnamed x13, local copies, waits for them, and re-layouts  80.5 us
    reshape x1, local copies, waits for them, and re-layouts, shards(): blocks = matrix.reshape(local_rows, NB, local_cols, NB)  78.7 us
    reshape x1, local copies, waits for them, and re-layouts, shards(): return blocks.reshape(matrix.shape)  78.2 us
  transfers between devices with their start and end apart: 6, of which 5 were waited for; matrix products, arithmetic and copies ran while one was open for 8% of the time, Pallas kernels for 0%

commit v1 on v0

--- a/solution.py
+++ b/solution.py
@@ -2,14 +2,20 @@
 import jax.numpy as jnp
 from jax import lax
 from jax.sharding import PartitionSpec as P
+from jax.lax import all_gather
 
 NB = 512
 STEPS = 2
 
 
+def detail_chains(array_here, axis_name):
+    f_now = all_gather(array_here, axis_name).sum(axis=0)
+    return f_now
+
+
 def spread(value, axis, source):
     kept = jnp.where(lax.axis_index(axis) == source, value, 0).astype(value.dtype)
-    return lax.psum(kept, axis)
+    return detail_chains(kept, axis)
 
 
 def trailing_product(column_panel, transposed):

time: 1580 us -> 1720 us (1.089)
  waiting for transfers between devices: 745 us -> 925 us
  local copies, waits for them, and re-layouts: 321 us -> 261 us
  other arithmetic: 302 us -> 330 us
    all_gather x0 -> x4, waiting for transfers between devices: none -> 428 us  [detail_chains(): f_now = all_gather(array_here, axis_name).sum(axis=0)]
    psum x4 -> x0, waiting for transfers between devices: 239 us -> none  [spread(): return lax.psum(kept, axis)]
    reshape x1 -> x0, local copies, waits for them, and re-layouts: 78.7 us -> none  [shards(): blocks = matrix.reshape(local_rows, NB, local_cols, NB)]
    reduce_sum x0 -> x4, other arithmetic: none -> 29.7 us  [detail_chains(): f_now = all_gather(array_here, axis_name).sum(axis=0)]
    unnamed x13 -> x11, local copies, waits for them, and re-layouts: 80.5 us -> 89.1 us
  transfers between devices with their start and end apart: 6 -> 6, of which waited for: 5 -> 6; matrix products, arithmetic and copies ran while one was open for 8% -> 4% of each run, Pallas kernels for 0% -> 0%
where the time goes in v1:
time: 1720 us; the launch traced here: 1700 us
  waiting for transfers between devices  925 us (54%)
  other arithmetic  330 us (19%)
  local copies, waits for them, and re-layouts  261 us (15%)
  matrix products  152 us (9%)
  between operations  32.8 us (2%)
    psum x2, waiting for transfers between devices, shards(): gathered = lax.psum(filled, 'row')  497 us
    all_gather x4, waiting for transfers between devices, detail_chains(): f_now = all_gather(array_here, axis_name).sum(axis=0)  428 us
    another operation x29, other arithmetic, shards(): factor_local = jnp.linalg.cholesky(chosen)  158 us
    dot_general x2, matrix products, trailing_product(): jnp.einsum('tan,sbn->tasb', column_panel, transposed, precision=lax.Preci...  126 us
    unnamed x11, local copies, waits for them, and re-layouts  89.1 us
    another operation x5, other arithmetic, shards(): jax.scipy.linalg.solve_triangular(factor_diag_block, source.reshape(local...  78.9 us
    reshape x1, local copies, waits for them, and re-layouts, shards(): return blocks.reshape(matrix.shape)  78.2 us
  transfers between devices with their start and end apart: 6, of which 6 were waited for; matrix products, arithmetic and copies ran while one was open for 4% of the time, Pallas kernels for 0%

profile of v1, /device:TPU:0, one launch (start us, length us, event | category | flops | bytes accessed | tf_op | source)
XLA Modules:
  0.0 1702.8 jit_solution(8540946298519223806)
XLA Ops:
  6.5 78.2 %copy.32 = f32[4,1,512,8,1,512]{2,5,3,0,4,1:T(8,128)} copy(f32[4,1,512,8,1,512]{5,4,3,2,1,0:T(1,128)} %param.12) | data formatting | bytes 67108864 | tf_op args[0]
  87.9 11.7 cholesky.286
  110.3 11.7 cholesky.305
  122.0 10.0 custom-call.28
  132.7 11.7 cholesky.326
  155.6 11.7 cholesky.343
  201.2 111.7 %all-gather.11.cloned.1.call-done = f32[4096,512]{1,0:T(8,128)} async-done(((f32[512,512]{1,0:T(8,128)}), f32[4096,512]{1,0:T(8,128)}) %all-gather.11.cloned.1.call-update) | async-done | bytes 8388624 | tf_op jit(solution)/shard_map/all_gather | solution.py:12
  325.8 39.3 %custom-call.30 = f32[4,128,128]{1,2,0:T(8,128)S(1)} custom-call(f32[4,128,128]{2,1,0:T(8,128)S(1)} %get-tuple-element.69), custom_call_target="InvertDiagBlocksLowerTriangular" | custom-call | tf_op jit(solution)/shard_map/jit(_solve_triangular)/triangular_solve | solution.py:55
  389.0 104.1 %all-gather.7.cloned.1.call-done = f32[4,4,512,512]{3,2,1,0:T(8,128)} async-done(((f32[1,4,512,512]{3,2,1,0:T(8,128)}), f32[4,4,512,512]{3,2,1,0:T(8,128)}) %all-gather.7.cloned.1.call-update) | async-done | bytes 16777232 | tf_op jit(solution)/shard_map/all_gather | solution.py:12
  493.2 10.4 reduce_sum.41
  547.5 248.6 %all-reduce.4.cloned.1.call-done = f32[8,512,512]{2,1,0:T(8,128)} async-done(((f32[8,512,512]{2,1,0:T(8,128)}), f32[8,512,512]{2,1,0:T(8,128)}) %all-reduce.4.cloned.1.call-update) | async-done | bytes 8388624 | tf_op jit(solution)/shard_map/psum | solution.py:68
  796.0 63.0 %convolution_subtract_fusion = f32[4,512,8,512]{1,3,2,0:T(8,128)} fusion(f32[4,512,8,512]{1,3,2,0:T(8,128)} %fusion.1, f32[8,512,512]{2,1,0:T(8,128)} %all-reduce.4.cloned.1.call-done, f32[4,512,512,1]{1,0,2,3:T(4,128)} %bitcast.153), kind=kOutput, calls=%fused_computation.5 | convolution fusion | flops 51547996160 | bytes 79691776 | tf_op jit(solution)/shard_map/tan,sbn->tasb/dot_general | solution.py:22
  862.1 11.7 cholesky.358
  884.5 11.7 cholesky.377
  897.6 10.2 custom-call.32
  908.5 11.7 cholesky.398
  931.3 11.7 cholesky.415
  963.1 108.2 %all-gather.13.cloned.1.call-done = f32[4096,512]{1,0:T(8,128)} async-done(((f32[512,512]{1,0:T(8,128)}), f32[4096,512]{1,0:T(8,128)}) %all-gather.13.cloned.1.call-update) | async-done | bytes 8388624 | tf_op jit(solution)/shard_map/all_gather | solution.py:12
  1084.1 39.3 %custom-call.34 = f32[4,128,128]{1,2,0:T(8,128)S(1)} custom-call(f32[4,128,128]{2,1,0:T(8,128)S(1)} %get-tuple-element.70), custom_call_target="InvertDiagBlocksLowerTriangular" | custom-call | tf_op jit(solution)/shard_map/jit(_solve_triangular)/triangular_solve | solution.py:55
  1147.6 104.0 %all-gather.9.cloned.1.call-done = f32[4,4,512,512]{3,2,1,0:T(8,128)} async-done(((f32[1,4,512,512]{3,2,1,0:T(8,128)}), f32[4,4,512,512]{3,2,1,0:T(8,128)}) %all-gather.9.cloned.1.call-update) | async-done | bytes 16777232 | tf_op jit(solution)/shard_map/all_gather | solution.py:12
  1251.5 10.3 reduce_sum.44
  1305.5 248.8 %all-reduce.6.cloned.1.call-done = f32[8,512,512]{2,1,0:T(8,128)} async-done(((f32[8,512,512]{2,1,0:T(8,128)}), f32[8,512,512]{2,1,0:T(8,128)}) %all-reduce.6.cloned.1.call-update) | async-done | bytes 8388624 | tf_op jit(solution)/shard_map/psum | solution.py:68
  1554.3 63.0 %subtract_bitcast_fusion = f32[4,1,512,8,1,512]{2,5,3,0,4,1:T(8,128)} fusion(f32[4,512,8,512]{1,3,2,0:T(8,128)} %fusion, f32[8,512,512]{2,1,0:T(8,128)} %all-reduce.6.cloned.1.call-done, f32[4,512,512,1]{1,0,2,3:T(4,128)} %bitcast.154), kind=kOutput, calls=%fused_computation.4 | convolution fusion | flops 51547996160 | bytes 79691776 | tf_op jit(solution)/shard_map/tan,sbn->tasb/dot_general | solution.py:22
  1617.3 78.2 %copy.53 = f32[4,1,512,8,1,512]{5,4,3,2,1,0:T(1,128)} copy(f32[4,1,512,8,1,512]{2,5,3,0,4,1:T(8,128)} %subtract_bitcast_fusion) | data formatting | bytes 67108864 | tf_op jit(solution)/shard_map/reshape | solution.py:89
  (151 shorter events, 265.1 us)
Async XLA Ops:
  6.5 306.4 %all-gather.11.cloned.1.call-start = ((), (), s32[]{:S(2)}) async-start(), calls=%async_computation.4 | async-start | bytes 9437184 | tf_op jit(solution)/shard_map/all_gather | solution.py:12
  185.6 307.6 %all-gather.7.cloned.1.call-start = ((), (), s32[]{:S(2)}) async-start(), calls=%async_computation | async-start | bytes 20971520 | tf_op jit(solution)/shard_map/all_gather | solution.py:12
  365.1 5.7 copy-start.2
  388.9 407.1 %all-reduce.4.cloned.1.call-start = ((), (), s32[]{:S(2)}) async-start(), calls=%async_computation.1 | async-start | bytes 16777216 | tf_op jit(solution)/shard_map/psum | solution.py:68
  519.3 4.3 copy-start.1
  526.0 545.3 %all-gather.13.cloned.1.call-start = ((), (), s32[]{:S(2)}) async-start(), calls=%async_computation.5 | async-start | bytes 9437184 | tf_op jit(solution)/shard_map/all_gather | solution.py:12
  947.6 303.9 %all-gather.9.cloned.1.call-start = ((), (), s32[]{:S(2)}) async-start(), calls=%async_computation.2 | async-start | bytes 20971520 | tf_op jit(solution)/shard_map/all_gather | solution.py:12
  1123.4 5.7 copy-start.3
  1147.3 407.0 %all-reduce.6.cloned.1.call-start = ((), (), s32[]{:S(2)}) async-start(), calls=%async_computation.3 | async-start | bytes 16777216 | tf_op jit(solution)/shard_map/psum | solution.py:68
  1277.6 4.3 copy-start
Sparse Core Ops, SparseCore 0:
  185.7 127.2 all-gather.10
  389.1 104.0 all-gather.6
  526.1 269.8 all-reduce.3
  947.7 123.5 all-gather.12
  1147.4 104.0 all-gather.8
  1284.4 269.8 all-reduce.5
